TPU v7x, 32 devices: a whole 2x2x4 slice. The times are simulated.
32 devices in a mesh: row: 4 (over y, core), col: 8 (over z, x).
Axes of the slice: x: 2, y: 2, z: 4, core: 2. Of those that a mesh axis runs over, the one named last changes fastest.
Arguments:
- x_blocks: bfloat16 [4, 8, 21, 128, 128], P('row', 'col'), may hold values from -1.1953125 to 1.1953125
- x_slots: int32 [4, 8, 21], replicated, may hold values from 0 to 127, as said below
- x_count: int32 [4, 8], replicated, may hold values from 10 to 21, as said below
- s_slots: int32 [4, 8, 2], replicated, may hold values from 0 to 15, as said below
- s_count: int32 [4, 8], replicated, may hold values from 1 to 2, as said below
Outputs:
- square_blocks: bfloat16 [4, 8, 2, 128, 128], P('row', 'col')
- result_blocks: bfloat16 [4, 8, 2, 128, 128], P('row', 'col')
Inputs may be any that keep to these rules, and one draw needn't show every extreme that they name: `x_slots`: in each tile the live slots hold distinct positions; the live blocks whose position % 16 is below 2 come first among the live slots, at most 2 of them, and some tile has exactly 2. Positions of slots that are not live are arbitrary within the range. `x_count`: some tile has exactly 21 live slots. `s_slots`: in each tile the live slots hold distinct positions. `s_count`: some tile has exactly 2 live slots.
All inputs are finite; a program needn't handle non-finite values.
Results may differ from a plain program's by a relative error of at most 0.0049.
Values may be sent and summed in bfloat16 or wider, within the bound.
No kernel may reach another device: no remote copies, remote signals or barrier semaphores. Data moves between devices by JAX's collectives and lax.ppermute only.
A program may use at most 128 MiB of HBM per device.

v0:
```python
import math
import jax
import jax.numpy as jnp
from jax import lax
from jax.sharding import PartitionSpec as P

RB = 8
JW = 2
CAPW = 2


def match_index(targets, slot_keys, slot_live):
    matches = (targets[..., None] == slot_keys) & slot_live
    ordinal = jnp.arange(1, slot_keys.shape[0] + 1, dtype=jnp.int32)
    located = jnp.sum(jnp.where(matches, ordinal, 0), axis=-1)
    return jnp.where(located > 0, located - 1, slot_keys.shape[0])


def local(x_blocks, x_slots, x_count, s_slots, s_count):
    row_total = lax.axis_size("row")
    col_total = lax.axis_size("col")
    row_id = lax.axis_index("row")
    col_id = lax.axis_index("col")
    capacity = x_blocks.shape[2]
    block_size = x_blocks.shape[3]
    order_blocks = RB * col_total
    tile_width = order_blocks // row_total
    panel_all = lax.all_gather(x_blocks, "row", axis=0, tiled=True)
    stacked = panel_all.reshape(row_total * capacity, block_size, block_size)
    padded = jnp.concatenate(
        [stacked, jnp.zeros((1, block_size, block_size), stacked.dtype)], axis=0
    )
    column_slots = lax.dynamic_index_in_dim(x_slots, col_id, 1, keepdims=False)
    column_count = lax.dynamic_index_in_dim(x_count, col_id, 1, keepdims=False)
    ordinal = jnp.arange(capacity, dtype=jnp.int32)
    panel_live = (ordinal[None, :] < column_count[:, None]).reshape(-1)
    owners = jnp.arange(row_total, dtype=jnp.int32)[:, None]
    panel_keys = (
        column_slots // tile_width * order_blocks + owners * tile_width + column_slots % tile_width
    ).reshape(-1)
    row_lanes = jnp.arange(RB, dtype=jnp.int32)
    window_ids = jnp.arange(JW, dtype=jnp.int32)

    def accumulate(running, values, inner_row, inner_col, usable):
        picked = match_index(
            row_lanes[None, :] * order_blocks + inner_row[:, None], panel_keys, panel_live
        )
        left_part = jnp.take(padded, picked, axis=0)
        placing = ((inner_col[:, None] == window_ids[None, :]) & usable[:, None]).astype(
            values.dtype
        )
        placed = placing[:, :, None, None] * values[:, None, :, :]
        return running + jnp.einsum(
            "nrxy,njyz->rjxz", left_part, placed, preferred_element_type=jnp.float32
        )

    def make_step(slot_table, count_row, stride, column_limit):

        def fold_step(running, piece, offset):
            pieces = piece.shape[1]
            slot_count = piece.shape[2]
            positions = lax.dynamic_slice_in_dim(slot_table, offset, pieces, 0)[:, :slot_count]
            counts = lax.dynamic_slice_in_dim(count_row, offset, pieces, 0)
            owner_ids = offset + jnp.arange(pieces, dtype=jnp.int32)[:, None]
            inner_row = owner_ids * RB + positions // stride
            inner_col = positions % stride
            usable = (jnp.arange(slot_count, dtype=jnp.int32)[None, :] < counts[:, None]) & (
                inner_col < column_limit
            )
            values = piece.reshape(pieces * slot_count, block_size, block_size)
            return accumulate(
                running, values, inner_row.reshape(-1), inner_col.reshape(-1), usable.reshape(-1)
            )

        return fold_step

    blank_sum = jnp.zeros((RB, JW, block_size, block_size), jnp.float32)

    def collect_all(gathered, fold_step):
        per_turn = math.gcd(col_total, 8)

        def advance(turn_index, running):
            offset = turn_index * per_turn
            portion = lax.dynamic_slice_in_dim(gathered, offset, per_turn, 1)
            return fold_step(running, portion, offset)

        return lax.fori_loop(0, col_total // per_turn, advance, blank_sum)

    row_slots = lax.dynamic_index_in_dim(x_slots, row_id, 0, keepdims=False)
    row_count = lax.dynamic_index_in_dim(x_count, row_id, 0, keepdims=False)
    square_slots = lax.dynamic_index_in_dim(s_slots, row_id, 0, keepdims=False)
    square_count = lax.dynamic_index_in_dim(s_count, row_id, 0, keepdims=False)
    window_part = x_blocks[:, :, :CAPW]
    first_step = make_step(row_slots, row_count, tile_width, JW)
    product = collect_all(lax.all_gather(window_part, "col", axis=1, tiled=True), first_step)
    own_slots = lax.dynamic_index_in_dim(square_slots, col_id, 0, keepdims=False)
    own_count = lax.dynamic_index_in_dim(square_count, col_id, 0, keepdims=False)
    own_live = jnp.arange(own_slots.shape[0], dtype=jnp.int32) < own_count
    flat_one = product.reshape(RB * JW, block_size, block_size)
    square_part = jnp.where(
        own_live[:, None, None], jnp.take(flat_one, own_slots, axis=0), 0.0
    ).astype(jnp.bfloat16)
    square_part = square_part[None, None]
    second_step = make_step(square_slots, square_count, JW, JW)
    second = collect_all(lax.all_gather(square_part, "col", axis=1, tiled=True), second_step)
    own_keys = own_slots // JW * order_blocks + row_id * tile_width + own_slots % JW
    own_block = jnp.take(padded, match_index(own_keys, panel_keys, panel_live), axis=0).astype(
        jnp.float32
    )
    flat_two = second.reshape(RB * JW, block_size, block_size)
    combined = 1.5 * own_block - 0.5 * jnp.take(flat_two, own_slots, axis=0)
    result = jnp.where(own_live[:, None, None], combined, 0.0).astype(jnp.bfloat16)
    return (square_part, result[None, None])


def solution(mesh):
    in_specs = (P("row", "col", None, None, None), P(), P(), P(), P())
    out_specs = (P("row", "col", None, None, None), P("row", "col", None, None, None))
    return jax.shard_map(local, mesh=mesh, in_specs=in_specs, out_specs=out_specs, check_vma=False)
```

profile of v0, /device:TPU:0, one launch (start us, length us, event | category | flops | bytes accessed | tf_op | source)
XLA Modules:
  0.0 114.3 jit_solution(4241437289012086558)
XLA Ops:
  7.2 0.7 all-gather.3.cloned.1.call-update
  8.0 0.9 dynamic-slice_reduce_fusion
  8.9 0.7 fusion.33
  9.6 0.7 constant_dynamic-slice_fusion.1
  10.2 0.9 fusion.30
  11.1 1.3 %dynamic_slice.43 = s32[1,1]{1,0:T(1,128)} dynamic-slice(s32[4,8]{1,0:T(4,128)} %param.13, s32[]{:T(128)S(6)} %select_n.191, s32[]{:T(128)S(6)} %select_n.193), dynamic_slice_sizes={1,1} | dynamic-slice | bytes 12 | tf_op jit(solution)/shard_map/jit(dynamic_index_in_dim)/dynamic_slice | solution.py:97
  12.9 0.1 squeeze.27
  13.2 0.1 lt.193
  13.4 0.7 select_reduce_fusion
  14.1 0.1 reshape.561
  14.2 0.1 and.203
  14.4 0.9 slice.19
  15.3 33.1 %all_gather.9 = bf16[1,8,2,128,128]{4,3,2,0,1:T(8,128)(2,1)S(1)} all-gather(bf16[1,1,2,128,128]{4,3,2,0,1:T(8,128)(2,1)S(1)} %slice.19), channel_id=1, replica_groups=mesh['row'=4,'col'=8] {'col'}, dimensions={1}, use_global_device_ids=true | all-gather | bytes 589824 | tf_op jit(solution)/shard_map/all_gather | solution.py:95
  48.4 0.3 copy.28
  48.9 0.1 lt.202
  49.0 0.2 fusion.29
  49.2 0.7 compare_and_fusion.2
  50.0 2.0 %concatenate.3 = bf16[85,128,128]{2,1,0:T(8,128)(2,1)S(1)} pad(bf16[84,128,128]{2,1,0:T(8,128)(2,1)} %bitcast.54, bf16[]{:T(256)} %constant.234.clone.1), padding=0_1x0_0x0_0 | pad | bytes 5537794 | tf_op jit(solution)/shard_map/concatenate | solution.py:30
  52.0 3.0 %gather_fusion.1 = bf16[128,128,128]{2,1,0:T(8,128)(2,1)} fusion(bf16[85,128,128]{2,1,0:T(8,128)(2,1)S(1)} %concatenate.3, s32[1024]{0:T(1024)S(1)} %pad_clamp_fusion.3), kind=kCustom, calls=%fused_computation.clone | custom fusion | bytes 8389120 | tf_op jit(solution)/shard_map/while/body/eval_jaxpr/jit(_take)/gather | solution.py:48
  55.0 4.4 %fusion.6 = bf16[8,2,128,128]{2,3,0,1:T(8,128)(2,1)} fusion(bf16[16,128,128]{1,2,0:T(8,128)(2,1)S(1)} %copy.28, bf16[16,2]{0,1:T(2,128)(2,1)S(1)} %and_convert_fusion.1, bf16[16,8,128,128]{3,2,1,0:T(8,128)(2,1)} %bitcast.52, pred[16,8]{1,0:T(8,128)(4,1)S(1)} %compare_and_fusion.1), kind=kOutput, calls=%fused_computation.13 | convolution fusion | flops 1077936128 | bytes 5243072 | tf_op jit(solution)/shard_map/while/body/eval_jaxpr/nrxy,njyz->rjxz/dot_general | solution.py:53
  59.3 1.3 %copy.30 = bf16[8,2,128,128]{3,2,1,0:T(8,128)(2,1)S(1)} copy(bf16[8,2,128,128]{2,3,0,1:T(8,128)(2,1)} %fusion.6) | data formatting | bytes 1048576 | tf_op jit(solution)/shard_map/while/body/eval_jaxpr/nrxy,njyz->rjxz/transpose | solution.py:53
  60.7 0.6 gather_fusion.2
  61.2 0.1 fusion.23
  61.3 0.7 fusion.37
  62.0 31.2 %all-gather = bf16[16,128,128]{2,1,0:T(8,128)(2,1)S(1)} all-gather(bf16[2,128,128]{2,1,0:T(8,128)(2,1)S(1)} %fusion.23), channel_id=2, replica_groups=mesh['row'=4,'col'=8] {'col'}, dimensions={0}, use_global_device_ids=true | all-gather | bytes 589824 | tf_op jit(solution)/shard_map/all_gather | solution.py:105
  93.3 1.0 copy.32
  94.3 3.0 %gather_fusion.3 = bf16[128,128,128]{2,1,0:T(8,128)(2,1)} fusion(bf16[85,128,128]{2,1,0:T(8,128)(2,1)S(1)} %concatenate.3, s32[1024]{0:T(1024)S(1)} %pad_clamp_fusion), kind=kCustom, calls=%fused_computation.2.clone | custom fusion | bytes 8389120 | tf_op jit(solution)/shard_map/while/body/eval_jaxpr/jit(_take)/gather | solution.py:48
  97.3 4.5 %fusion.9 = f32[8,2,128,128]{2,3,0,1:T(8,128)} fusion(bf16[16,128,128]{1,2,0:T(8,128)(2,1)S(1)} %copy-done.1, bf16[16,2]{0,1:T(2,128)(2,1)S(1)} %and_convert_fusion, bf16[16,8,128,128]{3,2,1,0:T(8,128)(2,1)} %bitcast.53, pred[16,8]{1,0:T(8,128)(4,1)S(1)} %compare_and_fusion), kind=kOutput, calls=%fused_computation.14 | convolution fusion | flops 1077936128 | bytes 5767360 | tf_op jit(solution)/shard_map/while/body/eval_jaxpr/nrxy,njyz->rjxz/dot_general | solution.py:53
  101.8 2.5 %copy.34 = f32[8,2,128,128]{3,2,1,0:T(8,128)} copy(f32[8,2,128,128]{2,3,0,1:T(8,128)} %fusion.9) | data formatting | bytes 2097152 | tf_op jit(solution)/shard_map/while/body/eval_jaxpr/nrxy,njyz->rjxz/transpose | solution.py:53
  104.3 1.8 %gather_fusion.4 = f32[2,128,128]{2,1,0:T(8,128)S(1)} fusion(f32[16,128,128]{2,1,0:T(8,128)} %bitcast.56, s32[1024]{0:T(1024)S(1)} %pad_clamp_fusion.2), kind=kCustom, calls=%fused_computation.3.clone | custom fusion | bytes 262152 | tf_op jit(solution)/shard_map/jit(_take)/gather | solution.py:111
  106.1 0.6 gather_fusion
  106.7 0.7 fusion.24
  (41 shorter events, 1.3 us)
Async XLA Ops:
  7.2 0.8 copy-start
  7.2 42.8 %all-gather.3.cloned.1.call-start = ((), (), s32[]{:S(2)}) async-start(), calls=%async_computation | async-start | bytes 3440640 | tf_op jit(solution)/shard_map/all_gather | solution.py:28
  94.3 3.0 %copy-start.1 = (bf16[16,128,128]{1,2,0:T(8,128)(2,1)S(1)}, bf16[16,128,128]{1,2,0:T(8,128)(2,1)}, u32[]{:S(2)}) copy-start(bf16[16,128,128]{1,2,0:T(8,128)(2,1)} %copy.32) | copy-start | bytes 1572868
Sparse Core Ops, SparseCore 0:
  9.5 28.9 all-gather.2
where the time goes:
time: 115 us; the launch traced here: 114 us
  blocking collectives  64.4 us (56%)
  local copies, waits for them, and re-layouts  22.5 us (20%)
  between operations  14.2 us (12%)
  matrix products  8.87 us (8%)
  other arithmetic  3.59 us (3%)
    all_gather x1, blocking collectives, local(): lax.all_gather(window_part, 'col', axis=1, tiled=True)  33.1 us
    all_gather x1, blocking collectives, local(): lax.all_gather(square_part, 'col', axis=1, tiled=True)  31.2 us
    dot_general x2, matrix products, accumulate(): jnp.einsum('nrxy,njyz->rjxz', left_part, placed, preferred_element_type=j...  8.87 us
    gather x2, local copies, waits for them, and re-layouts, accumulate(): left_part = jnp.take(padded, picked, axis=0)  6.02 us
    transpose x2, local copies, waits for them, and re-layouts, accumulate(): jnp.einsum('nrxy,njyz->rjxz', left_part, placed, preferred_element_type=j...  3.86 us
  transfers between devices with their start and end apart: 1, of which 0 were waited for; matrix products, arithmetic and copies ran while one was open for 8% of the time, Pallas kernels for 0%

commit v1 on v0

--- a/solution.py
+++ b/solution.py
@@ -102,7 +102,12 @@
     ).astype(jnp.bfloat16)
     square_part = square_part[None, None]
     second_step = make_step(square_slots, square_count, JW, JW)
-    second = collect_all(lax.all_gather(square_part, "col", axis=1, tiled=True), second_step)
+    second = collect_all(
+        jnp.concatenate(
+            lax.all_to_all(jnp.stack([square_part] * lax.axis_size("col")), "col", 0, 0), axis=1
+        ),
+        second_step,
+    )
     own_keys = own_slots // JW * order_blocks + row_id * tile_width + own_slots % JW
     own_block = jnp.take(padded, match_index(own_keys, panel_keys, panel_live), axis=0).astype(
         jnp.float32

time: 115 us -> 90.3 us (0.79)
  blocking collectives: 64.4 us -> 33.1 us
  waiting for transfers between devices: 0.7 us -> 6.55 us
  starting transfers between devices: 0.04 us -> 5.55 us
  local copies, waits for them, and re-layouts: 22.5 us -> 19.1 us
  matrix products: 8.87 us -> 7.63 us
    all_gather x1 -> x0, blocking collectives: 31.2 us -> none  [local(): lax.all_gather(square_part, 'col', axis=1, tiled=True)]
    all_to_all x0 -> x1, waiting for transfers between devices: none -> 5.85 us  [local(): lax.all_to_all(jnp.stack([square_part] * lax.axis_size('col')), 'col', 0, 0)]
    all_to_all x0 -> x1, starting transfers between devices: none -> 5.51 us  [local(): lax.all_to_all(jnp.stack([square_part] * lax.axis_size('col')), 'col', 0, 0)]
    transpose x2, local copies, waits for them, and re-layouts: 3.86 us -> 1.64 us  [accumulate(): jnp.einsum('nrxy,njyz->rjxz', left_part, placed, preferred_element_type=j...]
    dot_general x2, matrix products: 8.87 us -> 7.63 us  [accumulate(): jnp.einsum('nrxy,njyz->rjxz', left_part, placed, preferred_element_type=j...]
    gather x1, local copies, waits for them, and re-layouts: 1.78 us -> 0.56 us  [local(): combined = 1.5 * own_block - 0.5 * jnp.take(flat_two, own_slots, axis=0)]
  transfers between devices with their start and end apart: 1 -> 2, of which waited for: 0 -> 1; matrix products, arithmetic and copies ran while one was open for 8% -> 15% of each run, Pallas kernels for 0% -> 0%
where the time goes in v1:
time: 90.3 us; the launch traced here: 89.8 us
  blocking collectives  33.1 us (37%)
  local copies, waits for them, and re-layouts  19.1 us (21%)
  between operations  14.2 us (16%)
  matrix products  7.63 us (8%)
  waiting for transfers between devices  6.55 us (7%)
  starting transfers between devices  5.55 us (6%)
  other arithmetic  3.59 us (4%)
    all_gather x1, blocking collectives, local(): lax.all_gather(window_part, 'col', axis=1, tiled=True)  33.1 us
    dot_general x2, matrix products, accumulate(): jnp.einsum('nrxy,njyz->rjxz', left_part, placed, preferred_element_type=j...  7.63 us
    gather x2, local copies, waits for them, and re-layouts, accumulate(): left_part = jnp.take(padded, picked, axis=0)  6.02 us
    all_to_all x1, waiting for transfers between devices, local(): lax.all_to_all(jnp.stack([square_part] * lax.axis_size('col')), 'col', 0, 0)  5.85 us
    all_to_all x1, starting transfers between devices, local(): lax.all_to_all(jnp.stack([square_part] * lax.axis_size('col')), 'col', 0, 0)  5.51 us
    concatenate x1, local copies, waits for them, and re-layouts, local(): jnp.concatenate([stacked, jnp.zeros((1, block_size, block_size), stacked....  1.97 us
  transfers between devices with their start and end apart: 2, of which 1 were waited for; matrix products, arithmetic and copies ran while one was open for 15% of the time, Pallas kernels for 0%

profile of v1, /device:TPU:0, one launch (start us, length us, event | category | flops | bytes accessed | tf_op | source)
XLA Modules:
  0.0 89.8 jit_solution(16559252481376220606)
XLA Ops:
  7.2 0.7 all-gather.2.cloned.1.call-update
  8.0 0.7 fusion.33
  8.9 0.9 dynamic-slice_reduce_fusion
  9.8 1.3 %dynamic_slice.43 = s32[1,1]{1,0:T(1,128)} dynamic-slice(s32[4,8]{1,0:T(4,128)} %param.13, s32[]{:T(128)S(6)} %select_n.191, s32[]{:T(128)S(6)} %select_n.193), dynamic_slice_sizes={1,1} | dynamic-slice | bytes 12 | tf_op jit(solution)/shard_map/jit(dynamic_index_in_dim)/dynamic_slice | solution.py:97
  11.0 0.9 fusion.30
  11.9 0.7 constant_dynamic-slice_fusion.1
  12.9 0.1 squeeze.27
  13.3 0.1 lt.193
  13.5 0.7 select_reduce_fusion
  14.2 0.1 reshape.563
  14.4 0.9 slice.19
  15.3 33.1 %all_gather.6 = bf16[1,8,2,128,128]{4,3,2,0,1:T(8,128)(2,1)S(1)} all-gather(bf16[1,1,2,128,128]{4,3,2,0,1:T(8,128)(2,1)S(1)} %slice.19), channel_id=1, replica_groups=mesh['row'=4,'col'=8] {'col'}, dimensions={1}, use_global_device_ids=true | all-gather | bytes 589824 | tf_op jit(solution)/shard_map/all_gather | solution.py:95
  48.4 0.3 copy.28
  48.8 0.7 iota_compare_fusion.3
  49.5 0.2 fusion.29
  49.9 2.0 %concatenate.3 = bf16[85,128,128]{2,1,0:T(8,128)(2,1)S(1)} pad(bf16[84,128,128]{2,1,0:T(8,128)(2,1)} %bitcast.55, bf16[]{:T(256)} %constant.234.clone.1), padding=0_1x0_0x0_0 | pad | bytes 5537794 | tf_op jit(solution)/shard_map/concatenate | solution.py:30
  51.8 3.0 %gather_fusion.1 = bf16[128,128,128]{2,1,0:T(8,128)(2,1)} fusion(bf16[85,128,128]{2,1,0:T(8,128)(2,1)S(1)} %concatenate.3, s32[1024]{0:T(1024)S(1)} %pad_clamp_fusion.3), kind=kCustom, calls=%fused_computation.clone | custom fusion | bytes 8389120 | tf_op jit(solution)/shard_map/while/body/eval_jaxpr/jit(_take)/gather | solution.py:48
  54.8 4.3 %fusion.6 = bf16[8,2,128,128]{2,3,0,1:T(8,128)(2,1)} fusion(bf16[16,128,128]{1,2,0:T(8,128)(2,1)S(1)} %copy.28, bf16[16,2]{0,1:T(2,128)(2,1)S(1)} %and_convert_fusion.1, bf16[16,8,128,128]{3,2,1,0:T(8,128)(2,1)} %bitcast.54, pred[16,8]{1,0:T(8,128)(4,1)S(1)} %compare_and_fusion.1), kind=kOutput, calls=%fused_computation.13 | convolution fusion | flops 1077936128 | bytes 5243072 | tf_op jit(solution)/shard_map/while/body/eval_jaxpr/nrxy,njyz->rjxz/dot_general | solution.py:53
  59.2 1.3 %copy.30 = bf16[8,2,128,128]{3,2,1,0:T(8,128)(2,1)S(1)} copy(bf16[8,2,128,128]{2,3,0,1:T(8,128)(2,1)} %fusion.6) | data formatting | bytes 1048576 | tf_op jit(solution)/shard_map/while/body/eval_jaxpr/nrxy,njyz->rjxz/transpose | solution.py:53
  60.5 0.6 gather_fusion.2
  61.1 0.1 fusion.23
  61.2 0.1 copy.32
  61.3 0.9 %stack.3 = bf16[8,1,1,2,128,128]{4,5,3,2,1,0:T(8,128)(2,1)} broadcast(bf16[2,128,128]{1,2,0:T(8,128)(2,1)S(1)} %copy.32), dimensions={3,4,5} | broadcast | bytes 589824 | tf_op jit(solution)/shard_map/stack | solution.py:107
  62.2 5.5 %all-to-all-start = ((bf16[8,1,1,2,128,128]{4,5,3,2,1,0:T(8,128)(2,1)}), bf16[8,1,1,2,128,128]{4,5,3,2,1,0:T(8,128)(2,1)S(1)}, u32[]{:S(2)}, u32[]{:S(2)}) async-start(bf16[8,1,1,2,128,128]{4,5,3,2,1,0:T(8,128)(2,1)} %stack.3), calls=%async_computation | async-start | bytes 1048576 | tf_op jit(solution)/shard_map/all_to_all | solution.py:107
  67.8 3.0 %gather_fusion.3 = bf16[128,128,128]{2,1,0:T(8,128)(2,1)} fusion(bf16[85,128,128]{2,1,0:T(8,128)(2,1)S(1)} %concatenate.3, s32[1024]{0:T(1024)S(1)} %pad_clamp_fusion), kind=kCustom, calls=%fused_computation.2.clone | custom fusion | bytes 8389120 | tf_op jit(solution)/shard_map/while/body/eval_jaxpr/jit(_take)/gather | solution.py:48
  70.9 0.6 gather_fusion
  71.4 0.7 fusion.37
  72.1 5.8 %all-to-all-done = bf16[8,1,1,2,128,128]{4,5,3,2,1,0:T(8,128)(2,1)S(1)} async-done(((bf16[8,1,1,2,128,128]{4,5,3,2,1,0:T(8,128)(2,1)}), bf16[8,1,1,2,128,128]{4,5,3,2,1,0:T(8,128)(2,1)S(1)}, u32[]{:S(2)}, u32[]{:S(2)}) %all-to-all-start) | async-done | bytes 524320 | tf_op jit(solution)/shard_map/all_to_all | solution.py:107
  78.0 3.3 %fusion.9 = f32[8,2,128,128]{2,3,0,1:T(8,128)S(1)} fusion(bf16[16,128,128]{1,2,0:T(8,128)(2,1)S(1)} %bitcast.60, bf16[16,2]{0,1:T(2,128)(2,1)S(1)} %and_convert_fusion, bf16[16,8,128,128]{3,2,1,0:T(8,128)(2,1)} %bitcast.53, pred[16,8]{1,0:T(8,128)(4,1)S(1)} %compare_and_fusion), kind=kOutput, calls=%fused_computation.14 | convolution fusion | flops 1077936128 | bytes 5767360 | tf_op jit(solution)/shard_map/while/body/eval_jaxpr/nrxy,njyz->rjxz/dot_general | solution.py:53
  81.3 0.3 copy.34
  81.6 0.6 gather_fusion.4
  82.2 0.7 fusion.24
  (42 shorter events, 1.5 us)
Async XLA Ops:
  7.2 0.8 copy-start
  7.2 42.7 %all-gather.2.cloned.1.call-start = ((), (), s32[]{:S(2)}) async-start(), calls=%async_computation.1 | async-start | bytes 3440640 | tf_op jit(solution)/shard_map/all_gather | solution.py:28
  62.2 15.8 %all-to-all-start = ((bf16[8,1,1,2,128,128]{4,5,3,2,1,0:T(8,128)(2,1)}), bf16[8,1,1,2,128,128]{4,5,3,2,1,0:T(8,128)(2,1)S(1)}, u32[]{:S(2)}, u32[]{:S(2)}) async-start(bf16[8,1,1,2,128,128]{4,5,3,2,1,0:T(8,128)(2,1)} %stack.3), calls=%async_computation | async-start | bytes 1048576 | tf_op jit(solution)/shard_map/all_to_all | solution.py:107
Sparse Core Ops, SparseCore 0:
  9.5 28.9 all-gather.1
